TPU v7x, 32 devices: a whole 2x2x4 slice. The times are simulated.
32 devices in a mesh: mix: 4 (over z), span: 8 (over y, x, core).
Axes of the slice: x: 2, y: 2, z: 4, core: 2. Of those that a mesh axis runs over, the one named last changes fastest.
Arguments:
- mixture: bfloat16 [512, 256, 256], P(('mix', 'span')), parts along dimension 0, may hold values from -16 to 16, as said below
- w_query: bfloat16 [2, 256, 256], replicated, may hold values from -4 to 4
- w_key: bfloat16 [2, 256, 256], replicated, may hold values from -4 to 4
- w_value: bfloat16 [2, 256, 256], replicated, may hold values from -0.375 to 0.375
- w_out: bfloat16 [2, 256, 256], replicated, may hold values from -0.375 to 0.375
- w_up: bfloat16 [2, 256, 1024], replicated, may hold values from -0.375 to 0.375
- w_down: bfloat16 [2, 1024, 256], replicated, may hold values from -0.1875 to 0.1875
- ln_gain: float32 [2, 2, 256], replicated, may hold values from 0.25 to 1.75
- gln_gain: float32 [2, 256], replicated, may hold values from 0.25 to 1.75
- gln_bias: float32 [2, 256], replicated, may hold values from -3 to 3
Outputs:
- block_out: bfloat16 [512, 256, 256], P(('mix', 'span')), parts along dimension 0
There are 4 independent parts, one for each index of `mix`. A program takes and returns all parts, laid end to end along the dimension named above; an argument that names none is the same for every part. Nothing has to cross between parts.
Inputs may be any that keep to these rules, and one draw needn't show every extreme that they name: `mixture`: entries of order one, scaled by a factor per segment.
All inputs are finite; a program needn't handle non-finite values.
Results may differ from a plain program's by a relative error of at most 0.0057.
Values may be sent and summed in bfloat16 or wider, within the bound.
A program may use at most 128 MiB of HBM per device.

v0:
```python
import math

import jax
import jax.numpy as jnp
from jax import lax
from jax.sharding import PartitionSpec as P

D = 256
HEADS = 8


norm_eps = 1e-05


def pos_table(length, width):
    places = jnp.arange(length, dtype=jnp.float32)[:, None]
    column = jnp.arange(width)
    rates = jnp.exp(-(2 * (column // 2)).astype(jnp.float32) / width * math.log(10000.0))
    angles = places * rates[None, :]
    return jnp.where((column % 2 == 0)[None, :], jnp.sin(angles), jnp.cos(angles))


def norm_rows(rows, gain):
    center = jnp.mean(rows, axis=-1, keepdims=True)
    shifted = rows - center
    spread = jnp.mean(shifted * shifted, axis=-1, keepdims=True)
    return shifted * lax.rsqrt(spread + norm_eps) * gain


def group_width(count, length):
    best = 1
    for option in range(1, count + 1):
        if count % option == 0 and option * length <= max(512, length):
            best = option
    return best


def attend_block(queries, key_rows, values):
    head_dim = D // HEADS
    scores = jnp.einsum(
        "qbhd,kbhd->bhqk", queries, key_rows, preferred_element_type=jnp.float32
    ) / math.sqrt(head_dim)
    weights = jax.nn.softmax(scores, axis=-1).astype(jnp.bfloat16)
    context = jnp.einsum("bhqk,kbhd->qbhd", weights, values, preferred_element_type=jnp.float32)
    return context.astype(jnp.bfloat16)


def attend_along(queries, key_rows, values):
    length, count = (queries.shape[0], queries.shape[1])
    width = group_width(count, length)
    split_q = queries.reshape(length, count, HEADS, D // HEADS)
    split_k = key_rows.reshape(length, count, HEADS, D // HEADS)
    split_v = values.reshape(length, count, HEADS, D // HEADS)
    result = jnp.zeros(split_q.shape, jnp.bfloat16)

    def one_group(step, current):
        start = step * width
        block_q = lax.dynamic_slice_in_dim(split_q, start, width, 1)
        block_k = lax.dynamic_slice_in_dim(split_k, start, width, 1)
        block_v = lax.dynamic_slice_in_dim(split_v, start, width, 1)
        return lax.dynamic_update_slice_in_dim(
            current, attend_block(block_q, block_k, block_v), start, 1
        )

    result = lax.fori_loop(0, count // width, one_group, result)
    return result.reshape(length, count, D)


def encoder_layer(sequences, level, w_query, w_key, w_value, w_out, w_up, w_down, ln_gain):
    length, count = (sequences.shape[0], sequences.shape[1])
    inputs = sequences.astype(jnp.float32) + pos_table(length, D)[:, None, :]
    flat = inputs.reshape(length * count, D)
    normed = norm_rows(flat, ln_gain[level, 0]).astype(jnp.bfloat16)
    queries = jnp.dot(normed, w_query[level], preferred_element_type=jnp.float32).astype(
        jnp.bfloat16
    )
    key_rows = jnp.dot(normed, w_key[level], preferred_element_type=jnp.float32).astype(
        jnp.bfloat16
    )
    values = jnp.dot(normed, w_value[level], preferred_element_type=jnp.float32).astype(
        jnp.bfloat16
    )
    context = attend_along(
        queries.reshape(length, count, D),
        key_rows.reshape(length, count, D),
        values.reshape(length, count, D),
    )
    after_attn = flat + jnp.dot(
        context.reshape(length * count, D), w_out[level], preferred_element_type=jnp.float32
    )
    normed_two = norm_rows(after_attn, ln_gain[level, 1]).astype(jnp.bfloat16)
    hidden = jax.nn.relu(
        jnp.dot(normed_two, w_up[level], preferred_element_type=jnp.float32)
    ).astype(jnp.bfloat16)
    output = after_attn + jnp.dot(hidden, w_down[level], preferred_element_type=jnp.float32)
    return output.reshape(length, count, D)


def global_norm(rows, gain, bias, shards):
    cells_all = float(rows.size * shards)
    sums, squares = lax.psum((jnp.sum(rows), jnp.sum(rows * rows)), "span")
    center = sums / cells_all
    spread = squares / cells_all - center * center
    shifted = rows - center
    return gain * shifted * lax.rsqrt(spread + norm_eps) + bias


def body(mixture, w_query, w_key, w_value, w_out, w_up, w_down, ln_gain, gln_gain, gln_bias):
    shards = lax.axis_size("span")
    frames_first = jnp.swapaxes(mixture, 0, 1)
    intra_frames = encoder_layer(
        frames_first, 0, w_query, w_key, w_value, w_out, w_up, w_down, ln_gain
    )
    intra = jnp.swapaxes(intra_frames, 0, 1)
    intra_out = (
        global_norm(intra, gln_gain[0], gln_bias[0], shards) + mixture.astype(jnp.float32)
    ).astype(jnp.bfloat16)
    moved = lax.all_to_all(intra_out, "span", split_axis=1, concat_axis=0, tiled=True)
    inter = encoder_layer(moved, 1, w_query, w_key, w_value, w_out, w_up, w_down, ln_gain)
    final = (
        global_norm(inter, gln_gain[1], gln_bias[1], shards) + moved.astype(jnp.float32)
    ).astype(jnp.bfloat16)
    return lax.all_to_all(final, "span", split_axis=0, concat_axis=1, tiled=True)


def solution(mesh):
    in_specs = (P(("mix", "span"), None, None), P(), P(), P(), P(), P(), P(), P(), P(), P())
    out_specs = P(("mix", "span"), None, None)
    return jax.shard_map(body, mesh=mesh, in_specs=in_specs, out_specs=out_specs, check_vma=False)
```

profile of v0, /device:TPU:0, one launch (start us, length us, event | category | flops | bytes accessed | tf_op | source)
XLA Modules:
  0.0 442.6 jit_solution(13577876157406199121)
XLA Ops:
  1.0 3.0 bitcast_reduce_fusion
  4.0 3.4 convert_add_fusion.1
  7.4 5.4 %multiply_reduce_fusion.7 = f32[256,16]{1,0:T(8,128)S(1)} fusion(f32[256,16]{1,0:T(8,128)S(1)} %broadcast_multiply_fusion, f32[256,256]{1,0:T(8,128)S(1)} %cosine_select_fusion, bf16[16,256,256]{2,1,0:T(8,128)(2,1)S(1)} %copy-done.2), kind=kLoop, calls=%fused_computation.72 | loop fusion | flops 5238784 | bytes 2392064 | tf_op jit(solution)/shard_map/reduce_sum | solution.py:26
  12.8 3.7 multiply_convert_fusion.2
  18.6 10.0 %reshape_reshape.24 = bf16[256,16,8,32]{3,2,1,0:T(8,128)(2,1)} reshape(bf16[4096,256]{1,0:T(8,128)(2,1)} %convolution_convert_fusion.6) | data formatting | bytes 4194304 | tf_op jit(solution)/shard_map/reshape;reshape | solution.py:53
  28.6 10.0 %copy.26 = bf16[256,16,8,32]{0,3,2,1:T(8,128)(2,1)} copy(bf16[256,16,8,32]{3,2,1,0:T(8,128)(2,1)} %reshape_reshape.24) | data formatting | bytes 4194304 | tf_op jit(solution)/shard_map/while | solution.py:65
  40.6 10.0 %reshape_reshape.25 = bf16[256,16,8,32]{3,2,1,0:T(8,128)(2,1)} reshape(bf16[4096,256]{1,0:T(8,128)(2,1)} %convolution_convert_fusion.5) | data formatting | bytes 4194304 | tf_op jit(solution)/shard_map/reshape;reshape | solution.py:51
  50.6 10.0 %copy.27 = bf16[256,16,8,32]{0,3,2,1:T(8,128)(2,1)} copy(bf16[256,16,8,32]{3,2,1,0:T(8,128)(2,1)} %reshape_reshape.25) | data formatting | bytes 4194304 | tf_op jit(solution)/shard_map/while | solution.py:65
  62.7 10.0 %reshape_reshape.26 = bf16[256,16,8,32]{3,2,1,0:T(8,128)(2,1)} reshape(bf16[4096,256]{1,0:T(8,128)(2,1)} %convolution_convert_fusion.4) | data formatting | bytes 4194304 | tf_op jit(solution)/shard_map/reshape;reshape | solution.py:52
  72.7 10.0 %copy.28 = bf16[256,16,8,32]{0,3,2,1:T(8,128)(2,1)} copy(bf16[256,16,8,32]{3,2,1,0:T(8,128)(2,1)} %reshape_reshape.26) | data formatting | bytes 4194304 | tf_op jit(solution)/shard_map/while | solution.py:65
  82.9 58.2 %while.26 = (s32[]{:T(128)}, bf16[256,16,8,32]{0,3,2,1:T(8,128)(2,1)S(1)}, bf16[256,16,8,32]{0,3,2,1:T(8,128)(2,1)}, bf16[256,16,8,32]{0,3,2,1:T(8,128)(2,1)}, b...) while((s32[]{:T(128)}, bf16[256,16,8,32]{0,3,2,1:T(8,128)(2,1)S(1)}, ...), condition=%wide.region_5.6_spmd, body=%wide.region_2.5_spmd.sunk | while | flops 139591936 | bytes 9472139 | solution.py:65
  83.1 4.5 %fusion.156 = (f32[2,8,256]{2,1,0:T(8,128)S(1)}, f32[2,8,256,256]{2,3,1,0:T(8,128)}) fusion(bf16[256,16,8,32]{0,3,2,1:T(8,128)(2,1)} %get-tuple-element.353, s32[]{:T(128)S(6)} %select_n.100, bf16[256,16,8,32]{0,3,2,1:T(8,128)(2,1)} %get-tuple-element.352), kind=kOutput, calls=%fused_computation.134.clone.1 | convolution fusion | flops 70254848 | bytes 4736000 | tf_op jit(solution)/shard_map/while/body/eval_jaxpr/sub | solution.py:43
  87.6 2.8 fusion.157
  90.4 4.5 %fusion.156 = (f32[2,8,256]{2,1,0:T(8,128)S(1)}, f32[2,8,256,256]{2,3,1,0:T(8,128)}) fusion(bf16[256,16,8,32]{0,3,2,1:T(8,128)(2,1)} %get-tuple-element.353, s32[]{:T(128)S(6)} %select_n.100, bf16[256,16,8,32]{0,3,2,1:T(8,128)(2,1)} %get-tuple-element.352), kind=kOutput, calls=%fused_computation.134.clone.1 | convolution fusion | flops 70254848 | bytes 4736000 | tf_op jit(solution)/shard_map/while/body/eval_jaxpr/sub | solution.py:43
  94.9 2.7 fusion.157
  97.6 4.5 %fusion.156 = (f32[2,8,256]{2,1,0:T(8,128)S(1)}, f32[2,8,256,256]{2,3,1,0:T(8,128)}) fusion(bf16[256,16,8,32]{0,3,2,1:T(8,128)(2,1)} %get-tuple-element.353, s32[]{:T(128)S(6)} %select_n.100, bf16[256,16,8,32]{0,3,2,1:T(8,128)(2,1)} %get-tuple-element.352), kind=kOutput, calls=%fused_computation.134.clone.1 | convolution fusion | flops 70254848 | bytes 4736000 | tf_op jit(solution)/shard_map/while/body/eval_jaxpr/sub | solution.py:43
  102.1 2.8 fusion.157
  104.9 4.5 %fusion.156 = (f32[2,8,256]{2,1,0:T(8,128)S(1)}, f32[2,8,256,256]{2,3,1,0:T(8,128)}) fusion(bf16[256,16,8,32]{0,3,2,1:T(8,128)(2,1)} %get-tuple-element.353, s32[]{:T(128)S(6)} %select_n.100, bf16[256,16,8,32]{0,3,2,1:T(8,128)(2,1)} %get-tuple-element.352), kind=kOutput, calls=%fused_computation.134.clone.1 | convolution fusion | flops 70254848 | bytes 4736000 | tf_op jit(solution)/shard_map/while/body/eval_jaxpr/sub | solution.py:43
  109.4 2.7 fusion.157
  112.1 4.5 %fusion.156 = (f32[2,8,256]{2,1,0:T(8,128)S(1)}, f32[2,8,256,256]{2,3,1,0:T(8,128)}) fusion(bf16[256,16,8,32]{0,3,2,1:T(8,128)(2,1)} %get-tuple-element.353, s32[]{:T(128)S(6)} %select_n.100, bf16[256,16,8,32]{0,3,2,1:T(8,128)(2,1)} %get-tuple-element.352), kind=kOutput, calls=%fused_computation.134.clone.1 | convolution fusion | flops 70254848 | bytes 4736000 | tf_op jit(solution)/shard_map/while/body/eval_jaxpr/sub | solution.py:43
  116.6 2.8 fusion.157
  119.4 4.5 %fusion.156 = (f32[2,8,256]{2,1,0:T(8,128)S(1)}, f32[2,8,256,256]{2,3,1,0:T(8,128)}) fusion(bf16[256,16,8,32]{0,3,2,1:T(8,128)(2,1)} %get-tuple-element.353, s32[]{:T(128)S(6)} %select_n.100, bf16[256,16,8,32]{0,3,2,1:T(8,128)(2,1)} %get-tuple-element.352), kind=kOutput, calls=%fused_computation.134.clone.1 | convolution fusion | flops 70254848 | bytes 4736000 | tf_op jit(solution)/shard_map/while/body/eval_jaxpr/sub | solution.py:43
  123.9 2.7 fusion.157
  126.6 4.5 %fusion.156 = (f32[2,8,256]{2,1,0:T(8,128)S(1)}, f32[2,8,256,256]{2,3,1,0:T(8,128)}) fusion(bf16[256,16,8,32]{0,3,2,1:T(8,128)(2,1)} %get-tuple-element.353, s32[]{:T(128)S(6)} %select_n.100, bf16[256,16,8,32]{0,3,2,1:T(8,128)(2,1)} %get-tuple-element.352), kind=kOutput, calls=%fused_computation.134.clone.1 | convolution fusion | flops 70254848 | bytes 4736000 | tf_op jit(solution)/shard_map/while/body/eval_jaxpr/sub | solution.py:43
  131.1 2.8 fusion.157
  133.9 4.5 %fusion.156 = (f32[2,8,256]{2,1,0:T(8,128)S(1)}, f32[2,8,256,256]{2,3,1,0:T(8,128)}) fusion(bf16[256,16,8,32]{0,3,2,1:T(8,128)(2,1)} %get-tuple-element.353, s32[]{:T(128)S(6)} %select_n.100, bf16[256,16,8,32]{0,3,2,1:T(8,128)(2,1)} %get-tuple-element.352), kind=kOutput, calls=%fused_computation.134.clone.1 | convolution fusion | flops 70254848 | bytes 4736000 | tf_op jit(solution)/shard_map/while/body/eval_jaxpr/sub | solution.py:43
  138.4 2.7 fusion.157
  141.1 12.0 %copy.29 = bf16[256,16,8,32]{3,2,1,0:T(8,128)(2,1)} copy(bf16[256,16,8,32]{0,3,2,1:T(8,128)(2,1)S(1)} %get-tuple-element.193) | data formatting | bytes 4194304 | tf_op jit(solution)/shard_map/while | solution.py:65
  153.1 9.8 %reshape_reshape.27 = bf16[4096,256]{1,0:T(8,128)(2,1)S(1)} reshape(bf16[256,16,8,32]{3,2,1,0:T(8,128)(2,1)} %copy.29) | data formatting | bytes 4194304 | tf_op jit(solution)/shard_map/reshape;reshape | solution.py:89
  162.9 3.0 fusion.129
  169.2 10.3 %multiply_reduce_fusion.5 = (f32[]{:T(128)}, f32[]{:T(128)}, f32[4096,256]{1,0:T(8,128)}) fusion(f32[4096,256]{1,0:T(8,128)} %copy-done.5, bf16[2,1024,256]{2,1,0:T(8,128)(2,1)S(1)} %copy-done.13, f32[256]{0:T(256)S(1)} %bitcast.151, f32[4096]{0:T(1024)S(1)} %add_rsqrt_fusion.3, f32[4096]{0:T(1024)S(1)} %broadcast_multiply_fusion.3, ...), kind=kOutput, calls=%fused_computation.68 | convolution fusion | flops 4311744512 | bytes 13665288 | tf_op jit(solution)/shard_map/dot_general | solution.py:95
  179.5 15.8 %all-reduce.1 = (f32[]{:T(128)}, f32[]{:T(128)}) all-reduce(f32[]{:T(128)} %get-tuple-element.218, f32[]{:T(128)} %get-tuple-element.217), channel_id=1, replica_groups=mesh['mix'=4,'span'=8] {'span'}, use_global_device_ids=true, to_apply=%region_9.10 | all-reduce | flops 2 | bytes 16 | tf_op jit(solution)/shard_map/psum | solution.py:101
  197.9 2.6 broadcast_subtract_fusion.1
  200.7 3.0 fusion.55
  203.8 3.8 all-to-all-start
  208.6 25.5 %all-to-all-done = bf16[16,256,256]{2,0,1:T(8,128)(2,1)S(1)} async-done(((bf16[16,256,256]{2,0,1:T(8,128)(2,1)}), bf16[16,256,256]{2,0,1:T(8,128)(2,1)S(1)}, u32[]{:S(2)}, u32[]{:S(2)}) %all-to-all-start) | async-done | bytes 2097184 | tf_op jit(solution)/shard_map/all_to_all | solution.py:118
  234.7 2.4 fusion.61
  237.1 3.0 multiply_reduce_fusion.4
  247.6 2.6 bitcast_add_fusion.2
  250.2 10.0 %reshape_reshape.28 = bf16[128,32,8,32]{3,2,1,0:T(8,128)(2,1)} reshape(bf16[4096,256]{1,0:T(8,128)(2,1)} %convolution_convert_fusion.3) | data formatting | bytes 4194304 | tf_op jit(solution)/shard_map/reshape;reshape | solution.py:53
  260.2 11.1 %copy.31 = bf16[128,32,8,32]{0,3,2,1:T(8,128)(2,1)} copy(bf16[128,32,8,32]{3,2,1,0:T(8,128)(2,1)} %reshape_reshape.28) | data formatting | bytes 4194304 | tf_op jit(solution)/shard_map/while | solution.py:65
  271.3 10.0 %reshape_reshape.29 = bf16[128,32,8,32]{3,2,1,0:T(8,128)(2,1)} reshape(bf16[4096,256]{1,0:T(8,128)(2,1)} %convolution_convert_fusion.2) | data formatting | bytes 4194304 | tf_op jit(solution)/shard_map/reshape;reshape | solution.py:51
  281.3 11.3 %copy.32 = bf16[128,32,8,32]{0,3,2,1:T(8,128)(2,1)} copy(bf16[128,32,8,32]{3,2,1,0:T(8,128)(2,1)} %reshape_reshape.29) | data formatting | bytes 4194304 | tf_op jit(solution)/shard_map/while | solution.py:65
  292.6 6.2 %reshape_reshape.30 = bf16[128,32,8,32]{3,2,1,0:T(8,128)(2,1)} reshape(bf16[4096,256]{1,0:T(8,128)(2,1)S(1)} %convolution_convert_fusion.1) | data formatting | bytes 4194304 | tf_op jit(solution)/shard_map/reshape;reshape | solution.py:52
  298.8 11.1 %copy.33 = bf16[128,32,8,32]{0,3,2,1:T(8,128)(2,1)} copy(bf16[128,32,8,32]{3,2,1,0:T(8,128)(2,1)} %reshape_reshape.30) | data formatting | bytes 4194304 | tf_op jit(solution)/shard_map/while | solution.py:65
  310.3 43.0 %while.27 = (s32[]{:T(128)}, bf16[128,32,8,32]{0,3,2,1:T(8,128)(2,1)S(1)}, bf16[128,32,8,32]{0,3,2,1:T(8,128)(2,1)}, bf16[128,32,8,32]{0,3,2,1:T(8,128)(2,1)}, b...) while((s32[]{:T(128)}, bf16[128,32,8,32]{0,3,2,1:T(8,128)(2,1)S(1)}, ...), condition=%wide.region_17.18_spmd, body=%wide.region_14.17_spmd.sunk | while | flops 69861504 | bytes 5277835 | solution.py:65
  310.4 3.3 fusion.161
  315.7 3.3 fusion.161
  319.0 2.1 fusion.162
  321.1 3.3 fusion.161
  326.5 3.3 fusion.161
  331.9 3.3 fusion.161
  335.2 2.1 fusion.162
  337.3 3.3 fusion.161
  342.6 3.3 fusion.161
  348.0 3.3 fusion.161
  353.4 11.7 %copy.34 = bf16[128,32,8,32]{3,2,1,0:T(8,128)(2,1)} copy(bf16[128,32,8,32]{0,3,2,1:T(8,128)(2,1)S(1)} %get-tuple-element.194) | data formatting | bytes 4194304 | tf_op jit(solution)/shard_map/while | solution.py:65
  365.1 9.7 %reshape_reshape.31 = bf16[4096,256]{1,0:T(8,128)(2,1)S(1)} reshape(bf16[128,32,8,32]{3,2,1,0:T(8,128)(2,1)} %copy.34) | data formatting | bytes 4194304 | tf_op jit(solution)/shard_map/reshape;reshape | solution.py:89
  374.9 3.0 fusion.132
  377.9 2.1 copy-done.4
  381.3 10.3 %multiply_reduce_fusion.2 = (f32[]{:T(128)}, f32[]{:T(128)}, f32[4096,256]{1,0:T(8,128)}) fusion(f32[4096,256]{1,0:T(8,128)} %copy-done.4, bf16[2,1024,256]{2,1,0:T(8,128)(2,1)S(1)} %copy-done.14, f32[256]{0:T(256)S(1)} %bitcast.150, f32[4096]{0:T(1024)S(1)} %add_rsqrt_fusion.2, f32[4096]{0:T(1024)S(1)} %broadcast_multiply_fusion.2, ...), kind=kOutput, calls=%fused_computation.64 | convolution fusion | flops 4311744512 | bytes 13665288 | tf_op jit(solution)/shard_map/dot_general | solution.py:95
  391.6 12.4 %all-reduce = (f32[]{:T(128)}, f32[]{:T(128)}) all-reduce(f32[]{:T(128)} %get-tuple-element.216, f32[]{:T(128)} %get-tuple-element.215), channel_id=1, replica_groups=mesh['mix'=4,'span'=8] {'span'}, use_global_device_ids=true, to_apply=%region_21.22 | all-reduce | flops 2 | bytes 16 | tf_op jit(solution)/shard_map/psum | solution.py:101
  406.6 2.6 broadcast_subtract_fusion
  411.5 29.3 %all_to_all.27 = bf16[128,32,256]{2,1,0:T(8,128)(2,1)S(1)} all-to-all(bf16[128,32,256]{2,1,0:T(8,128)(2,1)S(1)} %fusion.60), channel_id=1, replica_groups=mesh['mix'=4,'span'=8] {'span'}, dimensions={0} | all-to-all | bytes 4194304 | tf_op jit(solution)/shard_map/all_to_all | solution.py:123
  (69 shorter events, 38.0 us)
Async XLA Ops:
  0.0 3.9 copy-start.2
  4.0 8.9 %copy-start.10 = (f32[2,2,256]{2,1,0:T(2,128)S(1)}, f32[2,2,256]{2,1,0:T(2,128)}, u32[]{:S(2)}) copy-start(f32[2,2,256]{2,1,0:T(2,128)} %param.21) | copy-start | bytes 12292
  7.4 9.2 %copy-start.6 = (bf16[2,256,256]{2,1,0:T(8,128)(2,1)S(1)}, bf16[2,256,256]{2,1,0:T(8,128)(2,1)}, u32[]{:S(2)}) copy-start(bf16[2,256,256]{2,1,0:T(8,128)(2,1)} %param.17) | copy-start | bytes 786436
  28.6 10.0 %copy-start.7 = (bf16[2,256,256]{2,1,0:T(8,128)(2,1)S(1)}, bf16[2,256,256]{2,1,0:T(8,128)(2,1)}, u32[]{:S(2)}) copy-start(bf16[2,256,256]{2,1,0:T(8,128)(2,1)} %param.15) | copy-start | bytes 786436
  50.6 10.0 %copy-start.8 = (bf16[2,256,256]{2,1,0:T(8,128)(2,1)S(1)}, bf16[2,256,256]{2,1,0:T(8,128)(2,1)}, u32[]{:S(2)}) copy-start(bf16[2,256,256]{2,1,0:T(8,128)(2,1)} %param.16) | copy-start | bytes 786436
  153.1 9.8 %copy-start.9 = (bf16[2,256,256]{2,1,0:T(8,128)(2,1)S(1)}, bf16[2,256,256]{2,1,0:T(8,128)(2,1)}, u32[]{:S(2)}) copy-start(bf16[2,256,256]{2,1,0:T(8,128)(2,1)} %param.18) | copy-start | bytes 786436
  165.9 2.0 copy-start.5
  165.9 3.3 copy-start.13
  169.2 28.6 %copy-start.11 = (f32[2,256]{1,0:T(2,128)S(1)}, f32[2,256]{1,0:T(2,128)}, u32[]{:S(2)}) copy-start(f32[2,256]{1,0:T(2,128)} %param.23) | copy-start | bytes 6148
  169.2 28.6 %copy-start.12 = (f32[2,256]{1,0:T(2,128)S(1)}, f32[2,256]{1,0:T(2,128)}, u32[]{:S(2)}) copy-start(f32[2,256]{1,0:T(2,128)} %param.22) | copy-start | bytes 6148
  197.9 2.9 copy-start.3
  203.8 30.4 %all-to-all-start = ((bf16[16,256,256]{2,0,1:T(8,128)(2,1)}), bf16[16,256,256]{2,0,1:T(8,128)(2,1)S(1)}, u32[]{:S(2)}, u32[]{:S(2)}) async-start(bf16[16,256,256]{2,0,1:T(8,128)(2,1)} %fusion.55), calls=%async_computation | async-start | bytes 4194304 | tf_op jit(solution)/shard_map/all_to_all | solution.py:118
  241.0 6.7 %copy-start = (f32[16,8,32,256]{3,2,0,1:T(8,128)}, f32[16,8,32,256]{3,2,0,1:T(8,128)S(1)}, u32[]{:S(2)}) copy-start(f32[16,8,32,256]{3,2,0,1:T(8,128)S(1)} %copy.30) | copy-start | bytes 12582916
  377.9 2.1 copy-start.4
  377.9 3.5 copy-start.14
  377.9 3.5 copy-start.15
  406.6 3.5 copy-start.1
where the time goes:
time: 450 us; the launch traced here: 443 us
  local copies, waits for them, and re-layouts  171 us (38%)
  matrix products  138 us (31%)
  blocking collectives  57.5 us (13%)
  other arithmetic  40.2 us (9%)
  waiting for transfers between devices  25.5 us (6%)
  between operations  5.96 us (1%)
    while x8, local copies, waits for them, and re-layouts, attend_along(): result = lax.fori_loop(0, count // width, one_group, result)  87.2 us
    sub x16, matrix products, attend_block(): weights = jax.nn.softmax(scores, axis=-1).astype(jnp.bfloat16)  62 us
    dot_general x16, matrix products, attend_block(): jnp.einsum('bhqk,kbhd->qbhd', weights, values, preferred_element_type=jnp...  38.7 us
    all_to_all x1, blocking collectives, body(): lax.all_to_all(final, 'span', split_axis=0, concat_axis=1, tiled=True)  29.3 us
    psum x2, blocking collectives, global_norm(): sums, squares = lax.psum((jnp.sum(rows), jnp.sum(rows * rows)), 'span')  28.2 us
    all_to_all x1, waiting for transfers between devices, body(): lax.all_to_all(intra_out, 'span', split_axis=1, concat_axis=0, tiled=True)  25.5 us
    dot_general x2, matrix products, encoder_layer(): jnp.dot(hidden, w_down[level], preferred_element_type=jnp.float32)  20.6 us
    another operation x2, local copies, waits for them, and re-layouts, attend_along(): split_v = values.reshape(length, count, HEADS, D // HEADS)  20 us
  transfers between devices with their start and end apart: 1, of which 1 were waited for; matrix products, arithmetic and copies ran while one was open for 0% of the time, Pallas kernels for 0%

commit v1 on v0

v1 whole, which is shorter than its diff:
```python
import math

import jax
import jax.numpy as jnp
import numpy as np
from jax import lax
from jax.experimental import pallas as pl
from jax.experimental.pallas import tpu as pltpu
from jax.sharding import PartitionSpec as P

HEADS = 8
norm_eps = 1e-05
F32 = jnp.float32
BF16 = jnp.bfloat16


def pos_table(length, width):
    places = np.arange(length, dtype=np.float64)[:, None]
    column = np.arange(width)
    rates = np.exp(-(2 * (column // 2)) / width * math.log(10000.0))
    angles = places * rates[None, :]
    return np.where((column % 2 == 0)[None, :], np.sin(angles), np.cos(angles)).astype(np.float32)


def norm_rows(rows, gain):
    center = jnp.mean(rows, axis=-1, keepdims=True)
    shifted = rows - center
    spread = jnp.mean(shifted * shifted, axis=-1, keepdims=True)
    return shifted * lax.rsqrt(spread + norm_eps) * gain


def dot(a, b):
    return jnp.dot(a, b, preferred_element_type=F32)


def dot_nt(a, b):
    return lax.dot_general(a, b, (((1,), (1,)), ((), ())), preferred_element_type=F32)


def softmax_rows(scores, factor):
    top = jnp.max(scores, axis=-1, keepdims=True)
    powers = jnp.exp2((scores - top) * factor)
    return (powers * (1.0 / jnp.sum(powers, axis=-1, keepdims=True))).astype(BF16)


def attend(q, k, v):
    length, width = q.shape
    head_dim = width // HEADS
    factor = math.log2(math.e) / math.sqrt(head_dim)
    lane_head = lax.broadcasted_iota(jnp.int32, (1, width), 1) // head_dim

    def mask(test):
        return jnp.where(test, 1.0, 0.0).astype(BF16)

    total = None
    if length * 2 <= width and length % 128 == 0:
        half = HEADS // 2
        k_two = jnp.concatenate(
            [k * mask(lane_head < half), k * mask(lane_head >= half)], axis=0
        )
        for h in range(half):
            low, high = mask(lane_head == h), mask(lane_head == h + half)
            scores = dot_nt(q * (low + high), k_two)
            weights = jnp.concatenate(
                [softmax_rows(scores[:, :length], factor), softmax_rows(scores[:, length:], factor)],
                axis=1,
            )
            part = dot(weights, jnp.concatenate([v * low, v * high], axis=0))
            total = part if total is None else total + part
    else:
        for h in range(HEADS):
            own = mask(lane_head == h)
            weights = softmax_rows(dot_nt(q * own, k), factor)
            part = dot(weights, v * own)
            total = part if total is None else total + part
    return total.astype(BF16)


def layer_rows(x, count, level, refs):
    wq, wk, wv, wo, wu, wd, ln = refs
    length = x.shape[0] // count
    normed = norm_rows(x, ln[level, 0:1]).astype(BF16)
    q = dot(normed, wq[level]).astype(BF16)
    k = dot(normed, wk[level]).astype(BF16)
    v = dot(normed, wv[level]).astype(BF16)
    parts = []
    for g in range(count):
        rows = slice(g * length, (g + 1) * length)
        parts.append(attend(q[rows], k[rows], v[rows]))
    context = parts[0] if count == 1 else jnp.concatenate(parts, axis=0)
    after = x + dot(context, wo[level])
    normed = norm_rows(after, ln[level, 1:2]).astype(BF16)
    hidden = jnp.maximum(dot(normed, wu[level]), 0.0).astype(BF16)
    return after + dot(hidden, wd[level])


def fold(rows):
    return jnp.sum(rows.reshape(rows.shape[0] // 8, 8, rows.shape[1]), axis=0)


def layer_kernel(level, x_ref, pos_ref, *rest):
    refs, (out_ref, stat_ref) = rest[:7], rest[7:]
    count, length, width = x_ref.shape
    x = x_ref[...].astype(F32) + pos_ref[...][None]
    y = layer_rows(x.reshape(count * length, width), count, level, refs)
    out_ref[...] = y.astype(BF16).reshape(count, length, width)

    @pl.when(pl.program_id(0) == 0)
    def _():
        stat_ref[...] = jnp.zeros_like(stat_ref)

    stat_ref[0] += fold(y)
    stat_ref[1] += fold(y * y)


def run_layer(x, level, weights):
    total, length, width = x.shape
    count = max(1, min(total, 512 // length))
    pos = jnp.asarray(pos_table(length, width))
    whole = lambda a: pl.BlockSpec(a.shape, lambda i: (0,) * a.ndim)
    return pl.pallas_call(
        lambda *r: layer_kernel(level, *r),
        grid=(total // count,),
        out_shape=(
            jax.ShapeDtypeStruct(x.shape, BF16),
            jax.ShapeDtypeStruct((2, 8, width), F32),
        ),
        in_specs=[pl.BlockSpec((count, length, width), lambda i: (i, 0, 0)), whole(pos)]
        + [whole(w) for w in weights],
        out_specs=(
            pl.BlockSpec((count, length, width), lambda i: (i, 0, 0)),
            pl.BlockSpec((2, 8, width), lambda i: (0, 0, 0)),
        ),
        compiler_params=pltpu.CompilerParams(vmem_limit_bytes=60 * 2**20),
        name="layer%d" % level,
    )(x, pos, *weights)


def global_norm(rows, stats, gain, bias, shards):
    cells = float(rows.size * shards)
    sums = lax.psum(jnp.sum(stats, axis=(1, 2)), "span")
    center = sums[0] / cells
    spread = sums[1] / cells - center * center
    return gain * (rows.astype(F32) - center) * lax.rsqrt(spread + norm_eps) + bias


def body(mixture, wq, wk, wv, wo, wu, wd, ln, gln_gain, gln_bias):
    shards = lax.axis_size("span")
    weights = (wq, wk, wv, wo, wu, wd, ln)
    intra, stats = run_layer(mixture, 0, weights)
    intra_out = (
        global_norm(intra, stats, gln_gain[0], gln_bias[0], shards) + mixture.astype(F32)
    ).astype(BF16)
    moved = lax.all_to_all(intra_out, "span", split_axis=1, concat_axis=0, tiled=True)
    inter, stats = run_layer(jnp.swapaxes(moved, 0, 1), 1, weights)
    back = lax.all_to_all(inter, "span", split_axis=1, concat_axis=0, tiled=True)
    final = global_norm(back, stats, gln_gain[1], gln_bias[1], shards)
    return (jnp.swapaxes(final, 0, 1) + intra_out.astype(F32)).astype(BF16)


def solution(mesh):
    in_specs = (P(("mix", "span"), None, None), P(), P(), P(), P(), P(), P(), P(), P(), P())
    out_specs = P(("mix", "span"), None, None)
    return jax.shard_map(body, mesh=mesh, in_specs=in_specs, out_specs=out_specs, check_vma=False)
```

time: 450 us -> 176 us (0.39); the launches traced: 443 us -> 176 us
  local copies, waits for them, and re-layouts: 171 us -> 9.21 us
  matrix products: 138 us -> 0 us
  Pallas kernels: 0 us -> 71.3 us
  other arithmetic: 40.2 us -> 8.71 us
  waiting for transfers between devices: 25.5 us -> 0.01 us
  blocking collectives: 57.5 us -> 77 us
    while x8 -> x0, local copies, waits for them, and re-layouts: 87.2 us -> none  [attend_along(): result = lax.fori_loop(0, count // width, one_group, result)]
    dot_general x26 -> x0, matrix products: 76.2 us -> none  [the longest x16 38.7 us: attend_block(): jnp.einsum('bhqk,kbhd->qbhd', weights, values, preferred_element_type=jnp...]
    another operation x8 -> x0, local copies, waits for them, and re-layouts: 75.7 us -> none  [the longest x2 20 us: attend_along(): split_v = values.reshape(length, count, HEADS, D // HEADS)]
    pallas_call x0 -> x2, Pallas kernels: none -> 71.3 us  [run_layer(): pl.pallas_call(lambda *r: layer_kernel(level, *r), grid=(total // count,)...]
    sub x16 -> x0, matrix products: 62 us -> none  [attend_block(): weights = jax.nn.softmax(scores, axis=-1).astype(jnp.bfloat16)]
    all_to_all x1, waiting for transfers between devices: 25.5 us -> 0.01 us  [body(): lax.all_to_all(inter, 'span', split_axis=1, concat_axis=0, tiled=True)]
    psum x2, blocking collectives: 28.2 us -> 48 us  [global_norm(): sums = lax.psum(jnp.sum(stats, axis=(1, 2)), 'span')]
    reduce_sum x6 -> x2, other arithmetic: 16.4 us -> 0.91 us  [global_norm(): sums = lax.psum(jnp.sum(stats, axis=(1, 2)), 'span')]
  transfers between devices with their start and end apart: 1 -> 1, of which waited for: 1 -> 0; matrix products, arithmetic and copies ran while one was open for 0% -> 0% of each run, Pallas kernels for 0% -> 0%
where the time goes in v1:
time: 176 us
  blocking collectives  77 us (44%)
  Pallas kernels  71.3 us (41%)
  local copies, waits for them, and re-layouts  9.21 us (5%)
  other arithmetic  8.71 us (5%)
  between operations  4.92 us (3%)
  starting transfers between devices  4.34 us (2%)
    pallas_call x2, Pallas kernels, run_layer(): pl.pallas_call(lambda *r: layer_kernel(level, *r), grid=(total // count,)...  71.3 us
    psum x2, blocking collectives, global_norm(): sums = lax.psum(jnp.sum(stats, axis=(1, 2)), 'span')  48 us
    all_to_all x1, blocking collectives, body(): lax.all_to_all(intra_out, 'span', split_axis=1, concat_axis=0, tiled=True)  29 us
    all_to_all x1, starting transfers between devices, body(): lax.all_to_all(inter, 'span', split_axis=1, concat_axis=0, tiled=True)  4.34 us
    pallas_call x1, local copies, waits for them, and re-layouts, run_layer(): pl.pallas_call(lambda *r: layer_kernel(level, *r), grid=(total // count,)...  4.1 us
  transfers between devices with their start and end apart: 1, of which 0 were waited for; matrix products, arithmetic and copies ran while one was open for 0% of the time, Pallas kernels for 0%

profile of v1, /device:TPU:0, one launch (start us, length us, event | category | flops | bytes accessed | tf_op | source)
XLA Modules:
  0.0 175.5 jit_solution(14735251678684461468)
XLA Ops:
  0.0 0.0 copy-start.1
  0.0 0.8 fusion.3
  0.8 36.8 %layer0.1 = (bf16[16,256,256]{2,1,0:T(8,128)(2,1)}, f32[2,8,256]{2,1,0:T(8,128)}) custom-call(bf16[16,256,256]{2,1,0:T(8,128)(2,1)} %r_0_.1, f32[256,256]{1,0:T(8,128)} %constant.25.clone.r_1_, bf16[2,256,256]{2,1,0:T(8,128)(2,1)} %r_2_.3, bf16[2,256,256]{2,1,0:T(8,128)(2,1)} %r_3_.3, bf16[2,256,256]{2,1,0:T(8,128)(2,1)} %r_4_.3, bf16[2,256,256]{2,1,0:T(8,128)(2,1)} %r_5_.3, ...), custom_call_target="tpu_custom_call" | custom-call | tf_op jit(solution)/shard_map/layer0/pallas_call | solution.py:121
  37.6 0.8 reduce_sum.18
  38.4 0.0 copy-done.1
  38.4 15.1 %psum.14 = f32[2]{0:T(128)S(1)} all-reduce(f32[2]{0:T(128)S(1)} %reduce_sum.18), channel_id=1, replica_groups=mesh['mix'=4,'span'=8] {'span'}, use_global_device_ids=true, to_apply=%region_1.0 | all-reduce | flops 2 | bytes 16 | tf_op jit(solution)/shard_map/psum | solution.py:141
  53.6 0.6 fusion.6
  56.5 3.2 %add_convert_fusion = bf16[16,256,256]{2,1,0:T(8,128)(2,1)S(1)} fusion(bf16[16,256,256]{2,1,0:T(8,128)(2,1)} %r_0_.1, bf16[16,256,256]{2,1,0:T(8,128)(2,1)} %get-tuple-element.9, f32[256]{0:T(256)S(1)} %bitcast.35, f32[]{:T(128)} %bitcast.3, f32[]{:T(128)} %bitcast.2, f32[256]{0:T(256)S(1)} %bitcast.34), kind=kLoop, calls=%fused_computation.6 | loop fusion | flops 8388608 | bytes 6293512 | tf_op jit(solution)/shard_map/convert_element_type | solution.py:153
  59.8 1.2 copy.15
  61.0 29.0 %all_to_all.27 = bf16[16,256,256]{2,0,1:T(8,128)(2,1)S(1)} all-to-all(bf16[16,256,256]{2,0,1:T(8,128)(2,1)S(1)} %copy.15), channel_id=1, replica_groups=mesh['mix'=4,'span'=8] {'span'}, dimensions={1} | all-to-all | bytes 4194304 | tf_op jit(solution)/shard_map/all_to_all | solution.py:154
  90.0 1.6 copy.16
  91.6 34.5 %layer1.1 = (bf16[32,128,256]{2,1,0:T(8,128)(2,1)}, f32[2,8,256]{2,1,0:T(8,128)}) custom-call(bf16[32,128,256]{2,1,0:T(8,128)(2,1)} %bitcast.30, f32[128,256]{1,0:T(8,128)} %constant.26.clone.r_1_, bf16[2,256,256]{2,1,0:T(8,128)(2,1)} %r_2_.3, bf16[2,256,256]{2,1,0:T(8,128)(2,1)} %r_3_.3, bf16[2,256,256]{2,1,0:T(8,128)(2,1)} %r_4_.3, ...), custom_call_target="tpu_custom_call" | custom-call | tf_op jit(solution)/shard_map/layer1/pallas_call | solution.py:121
  126.0 0.0 copy-start
  126.0 4.1 %copy.17 = bf16[32,128,256]{2,0,1:T(8,128)(2,1)} copy(bf16[32,128,256]{2,1,0:T(8,128)(2,1)} %get-tuple-element.11) | data formatting | bytes 4194304 | tf_op jit(solution)/shard_map/layer1/pallas_call | solution.py:121
  130.1 4.3 %all-to-all-start.1 = ((bf16[32,128,256]{2,0,1:T(8,128)(2,1)}), bf16[32,128,256]{2,0,1:T(8,128)(2,1)}, u32[]{:S(2)}, u32[]{:S(2)}) async-start(bf16[32,128,256]{2,0,1:T(8,128)(2,1)} %copy.17), calls=%async_computation.1 | async-start | bytes 4194304 | tf_op jit(solution)/shard_map/all_to_all | solution.py:156
  134.5 0.0 copy-done
  134.5 0.1 reduce_sum.19
  134.6 32.9 %psum.15 = f32[2]{0:T(128)S(1)} all-reduce(f32[2]{0:T(128)S(1)} %reduce_sum.19), channel_id=1, replica_groups=mesh['mix'=4,'span'=8] {'span'}, use_global_device_ids=true, to_apply=%region_3.0 | all-reduce | flops 2 | bytes 16 | tf_op jit(solution)/shard_map/psum | solution.py:141
  167.5 0.6 fusion.5
  170.6 0.0 all-to-all-done.1
  170.6 2.2 %convert_subtract_fusion = f32[32,128,256]{2,0,1:T(8,128)S(1)} fusion(bf16[32,128,256]{2,0,1:T(8,128)(2,1)} %all-to-all-done.1, f32[]{:T(128)} %bitcast.9), kind=kLoop, calls=%fused_computation.5 | loop fusion | flops 2097152 | bytes 6291460 | tf_op jit(solution)/shard_map/sub | solution.py:144
  172.8 0.3 copy.18
  173.2 2.4 %fusion.2 = bf16[16,256,256]{2,1,0:T(8,128)(2,1)} fusion(bf16[16,256,256]{2,1,0:T(8,128)(2,1)S(1)} %add_convert_fusion, f32[256]{0:T(256)S(1)} %bitcast.33, f32[32,8,16,256]{3,0,1,2:T(8,128)S(1)} %copy.18, f32[]{:T(128)} %bitcast.13, f32[256]{0:T(256)S(1)} %bitcast.32), kind=kLoop, calls=%fused_computation.4 | loop fusion | flops 6291456 | bytes 8390660 | tf_op jit(solution)/shard_map/convert_element_type | solution.py:158
  (1 shorter events, 0.0 us)
Async XLA Ops:
  0.0 38.4 %copy-start.1 = (f32[2,256]{1,0:T(2,128)S(1)}, f32[2,256]{1,0:T(2,128)}, u32[]{:S(2)}) copy-start(f32[2,256]{1,0:T(2,128)} %param.21) | copy-start | bytes 6148
  126.0 8.4 %copy-start = (f32[2,8,256]{2,1,0:T(8,128)S(1)}, f32[2,8,256]{2,1,0:T(8,128)}, u32[]{:S(2)}) copy-start(f32[2,8,256]{2,1,0:T(8,128)} %get-tuple-element.12) | copy-start | bytes 49156
  130.1 40.5 %all-to-all-start.1 = ((bf16[32,128,256]{2,0,1:T(8,128)(2,1)}), bf16[32,128,256]{2,0,1:T(8,128)(2,1)}, u32[]{:S(2)}, u32[]{:S(2)}) async-start(bf16[32,128,256]{2,0,1:T(8,128)(2,1)} %copy.17), calls=%async_computation.1 | async-start | bytes 4194304 | tf_op jit(solution)/shard_map/all_to_all | solution.py:156

commit v2 on v1

--- a/solution.py
+++ b/solution.py
@@ -98,64 +98,306 @@
     return jnp.sum(rows.reshape(rows.shape[0] // 8, 8, rows.shape[1]), axis=0)
 
 
-def layer_kernel(level, x_ref, pos_ref, *rest):
-    refs, (out_ref, stat_ref) = rest[:7], rest[7:]
-    count, length, width = x_ref.shape
-    x = x_ref[...].astype(F32) + pos_ref[...][None]
-    y = layer_rows(x.reshape(count * length, width), count, level, refs)
-    out_ref[...] = y.astype(BF16).reshape(count, length, width)
-
-    @pl.when(pl.program_id(0) == 0)
-    def _():
-        stat_ref[...] = jnp.zeros_like(stat_ref)
-
-    stat_ref[0] += fold(y)
-    stat_ref[1] += fold(y * y)
-
-
-def run_layer(x, level, weights):
-    total, length, width = x.shape
-    count = max(1, min(total, 512 // length))
-    pos = jnp.asarray(pos_table(length, width))
-    whole = lambda a: pl.BlockSpec(a.shape, lambda i: (0,) * a.ndim)
-    return pl.pallas_call(
-        lambda *r: layer_kernel(level, *r),
-        grid=(total // count,),
-        out_shape=(
-            jax.ShapeDtypeStruct(x.shape, BF16),
-            jax.ShapeDtypeStruct((2, 8, width), F32),
+def peer_of(j, size):
+    return lax.rem(lax.axis_index("span") + j, size)
+
+
+def remote(src, dst, send_sem, recv_sem, peer):
+    return pltpu.make_async_remote_copy(
+        src_ref=src,
+        dst_ref=dst,
+        send_sem=send_sem,
+        recv_sem=recv_sem,
+        device_id={"span": peer},
+        device_id_type=pl.DeviceIdType.MESH,
+    )
+
+
+def lanes_of(ref, rows):
+    return jnp.concatenate([ref[c, rows, :] for c in range(ref.shape[0])], axis=1)
+
+
+def block_kernel(
+    n, halves, mix, wq_h, wk_h, wv_h, wo_h, wu_h, wd_h, ln, gain, bias, pos0, pos1, out,
+    mix_v, mix_got, y_own, y_got, x_two, z_own, z_got, z_wide,
+    wq, wk, wv, wo, wu, wd, stat, stat_own, stat_got,
+    w_sem, mix_sem, keep_sem, mix_send, mix_recv, y_send, y_recv, z_send, z_recv,
+    stat_send, stat_recv,
+):
+    me = lax.axis_index("span")
+    segs, _, span_rows, width = mix.shape
+    frames = n * halves * span_rows
+    long = n * segs
+    own_frames = halves * span_rows
+    two = max(1, min(segs, 512 // frames))
+    four = max(1, min(span_rows, 512 // long))
+    cells = float(long * frames * width)
+
+    loads = [
+        [
+            pltpu.make_async_copy(src.at[level], dst.at[level], w_sem.at[level, i])
+            for i, (src, dst) in enumerate(
+                ((wq_h, wq), (wk_h, wk), (wv_h, wv), (wo_h, wo), (wu_h, wu), (wd_h, wd))
+            )
+        ]
+        for level in range(2)
+    ]
+    first = pltpu.make_async_copy(mix.at[:two], mix_v.at[:two], mix_sem.at[0])
+    later = pltpu.make_async_copy(mix.at[two:], mix_v.at[two:], mix_sem.at[1])
+    first.start()
+    for load in loads[0]:
+        load.start()
+    later.start()
+
+    barrier = pltpu.get_barrier_semaphore()
+    for j in range(1, n):
+        pl.semaphore_signal(
+            barrier, inc=1, device_id={"span": peer_of(j, n)}, device_id_type=pl.DeviceIdType.MESH
+        )
+    pl.semaphore_wait(barrier, n - 1)
+
+    def mix_copy(j, half):
+        peer = peer_of(j, n)
+        return remote(
+            mix.at[:, peer * halves + half],
+            mix_got.at[half, pl.ds(me * segs, segs)],
+            mix_send.at[half, j],
+            mix_recv.at[half, j],
+            peer,
+        )
+
+    def keep_copy(half):
+        return pltpu.make_async_copy(
+            mix.at[:, me * halves + half],
+            mix_got.at[half, pl.ds(me * segs, segs)],
+            keep_sem.at[half],
+        )
+
+    for j in range(1, n):
+        mix_copy(j, 0).start()
+    for half in range(halves):
+        keep_copy(half).start()
+    for load in loads[1]:
+        load.start()
+
+    def y_copy(j, start, size):
+        peer = peer_of(j, n)
+        return remote(
+            y_own.at[pl.ds(start, size), pl.ds(peer * halves, halves)],
+            y_got.at[pl.ds(me * segs + start, size)],
+            y_send.at[j],
+            y_recv.at[j],
+            peer,
+        )
+
+    def z_copy(j, start, size):
+        peer = peer_of(j, n)
+        return remote(
+            z_own.at[pl.ds(start, size), peer],
+            z_got.at[pl.ds(me * own_frames + start, size)],
+            z_send.at[j],
+            z_recv.at[j],
+            peer,
+        )
+
+    def add_stats(rows):
+        stat[0] += fold(rows)
+        stat[1] += fold(rows * rows)
+
+    def share_stats(which):
+        total = jnp.sum(jnp.sum(stat[0], axis=0, keepdims=True), axis=1, keepdims=True)
+        square = jnp.sum(jnp.sum(stat[1], axis=0, keepdims=True), axis=1, keepdims=True)
+        row = lax.broadcasted_iota(jnp.int32, (8, 128), 0)
+        tile = jnp.where(row == 0, total, square)
+        stat_own[which] = tile
+        stat_got[which, me] = tile
+        stat[...] = jnp.zeros_like(stat)
+
+    def stat_copy(which, j):
+        return remote(
+            stat_own.at[which],
+            stat_got.at[which, me],
+            stat_send.at[which, j],
+            stat_recv.at[which, j],
+            peer_of(j, n),
+        )
+
+    def read_stats(which):
+        for j in range(1, n):
+            stat_copy(which, j).wait()
+        tile = jnp.sum(stat_got[which], axis=0)
+        center = tile[0:1, 0:1] / cells
+        spread = tile[1:2, 0:1] / cells - center * center
+        return center, lax.rsqrt(spread + norm_eps)
+
+    stat[...] = jnp.zeros_like(stat)
+    first.wait()
+    for load in loads[0]:
+        load.wait()
+    later.wait()
+    refs = (wq, wk, wv, wo, wu, wd, ln)
+
+    def intra_step(i, carry):
+        @pl.when(i > 0)
+        def _():
+            for j in range(1, n):
+                y_copy(j, (i - 1) * two, two).start()
+
+        x = mix_v[pl.ds(i * two, two)].astype(F32).reshape(two, frames, width) + pos0[...][None]
+        y = layer_rows(x.reshape(two * frames, width), two, 0, refs)
+        y_own[pl.ds(i * two, two)] = y.astype(BF16).reshape(two, n * halves, span_rows, width)
+        add_stats(y)
+        return carry
+
+    steps = segs // two
+    lax.fori_loop(0, steps, intra_step, 0)
+    share_stats(0)
+    for j in range(1, n):
+        stat_copy(0, j).start()
+    for j in range(1, n):
+        y_copy(j, (steps - 1) * two, two).start()
+    for half in range(1, halves):
+        for j in range(1, n):
+            mix_copy(j, half).start()
+
+    def keep_step(s, carry):
+        y_got[me * segs + s] = y_own[s, pl.ds(me * halves, halves)]
+        return carry
+
+    lax.fori_loop(0, segs, keep_step, 0)
+    for load in loads[1]:
+        load.wait()
+    center, scale = read_stats(0)
+
+    def mid(rows, mixture):
+        normed = gain[0:1] * (rows.astype(F32) - center) * scale + bias[0:1]
+        return (normed + mixture.astype(F32)).astype(BF16).astype(F32)
+
+    for j in range(1, n):
+        y_copy(j, 0, segs).wait_recv()
+
+    for half in range(halves):
+        keep_copy(half).wait()
+        for j in range(1, n):
+            mix_copy(j, half).wait_recv()
+
+        def turn_step(g, carry, half=half):
+            for t in range(8):
+                s = g * 8 + t
+                rows = mid(y_got[s, half], mix_got[half, s])
+                for c in range(width // 128):
+                    x_two[c, pl.ds(s, span_rows, stride=long), :] = rows[:, c * 128 : c * 128 + 128]
+            return carry
+
+        lax.fori_loop(0, long // 8, turn_step, 0)
+
+        def inter_step(i, carry, half=half):
+            here = half * span_rows + i * four
+
+            @pl.when(here > 0)
+            def _():
+                for j in range(1, n):
+                    z_copy(j, here - four, four).start()
+
+            x = lanes_of(x_two, pl.ds(i * four * long, four * long)).reshape(four, long, width)
+            x = x + pos1[...][None]
+            z = layer_rows(x.reshape(four * long, width), four, 1, refs)
+            z_own[pl.ds(here, four)] = z.astype(BF16).reshape(four, n, segs, width)
+            add_stats(z)
+            return carry
+
+        lax.fori_loop(0, span_rows // four, inter_step, 0)
+
+    share_stats(1)
+    for j in range(1, n):
+        stat_copy(1, j).start()
+    for j in range(1, n):
+        z_copy(j, own_frames - four, four).start()
+
+    def own_step(f, carry):
+        z_got[me * own_frames + f] = z_own[f, me]
+        return carry
+
+    lax.fori_loop(0, own_frames, own_step, 0)
+    center_two, scale_two = read_stats(1)
+    for j in range(1, n):
+        z_copy(j, 0, own_frames).wait_recv()
+
+    def widen_step(f, carry):
+        rows = z_got[pl.ds(f * 8, 8)].astype(F32).reshape(8 * segs, width)
+        for c in range(width // 128):
+            z_wide[c, pl.ds(f * 8 * segs, 8 * segs), :] = rows[:, c * 128 : c * 128 + 128]
+        return carry
+
+    lax.fori_loop(0, frames // 8, widen_step, 0)
+
+    def final_step(s, carry):
+        z = lanes_of(z_wide, pl.ds(s, frames, stride=segs))
+        normed = gain[1:2] * (z - center_two) * scale_two + bias[1:2]
+        shape = (frames, width)
+        across = mid(y_own[s].reshape(shape), mix_v[s].reshape(shape))
+        out[s] = (normed + across).astype(BF16).reshape(out.shape[1:])
+        return carry
+
+    lax.fori_loop(0, segs, final_step, 0)
+    for j in range(1, n):
+        for half in range(halves):
+            mix_copy(j, half).wait_send()
+        y_copy(j, 0, segs).wait_send()
+        z_copy(j, 0, own_frames).wait_send()
+
+
+def body(mixture, wq, wk, wv, wo, wu, wd, ln, gln_gain, gln_bias):
+    n = lax.axis_size("span")
+    segs, frames, width = mixture.shape
+    own = frames // n
+    halves = 2 if own % 32 == 0 else 1
+    rows = own // halves
+    long = n * segs
+    mix = mixture.reshape(segs, n * halves, rows, width)
+    pos0, pos1 = jnp.asarray(pos_table(frames, width)), jnp.asarray(pos_table(long, width))
+    anywhere = pl.BlockSpec(memory_space=pl.ANY)
+    vmem = pl.BlockSpec(memory_space=pltpu.VMEM)
+    dma = pltpu.SemaphoreType.DMA
+    weights = (wq, wk, wv, wo, wu, wd)
+    result = pl.pallas_call(
+        lambda *r: block_kernel(n, halves, *r),
+        out_shape=jax.ShapeDtypeStruct(mix.shape, BF16),
+        in_specs=[anywhere] * 7 + [vmem] * 5,
+        out_specs=vmem,
+        scratch_shapes=[
+            pltpu.VMEM(mix.shape, BF16),
+            pltpu.VMEM((halves, long, rows, width), BF16),
+            pltpu.VMEM(mix.shape, BF16),
+            pltpu.VMEM((long, halves, rows, width), BF16),
+            pltpu.VMEM((width // 128, rows * long, 128), F32),
+            pltpu.VMEM((own, n, segs, width), BF16),
+            pltpu.VMEM((frames, segs, width), BF16),
+            pltpu.VMEM((width // 128, frames * segs, 128), F32),
+        ]
+        + [pltpu.VMEM(w.shape, BF16) for w in weights]
+        + [
+            pltpu.VMEM((2, 8, width), F32),
+            pltpu.VMEM((2, 8, 128), F32),
+            pltpu.VMEM((2, n, 8, 128), F32),
+            dma((2, 6)),
+            dma((2,)),
+            dma((halves,)),
+            dma((halves, n)),
+            dma((halves, n)),
+            dma((n,)),
+            dma((n,)),
+            dma((n,)),
+            dma((n,)),
+            dma((2, n)),
+            dma((2, n)),
+        ],
+        compiler_params=pltpu.CompilerParams(
+            collective_id=0, has_side_effects=True, vmem_limit_bytes=62 * 2**20
         ),
-        in_specs=[pl.BlockSpec((count, length, width), lambda i: (i, 0, 0)), whole(pos)]
-        + [whole(w) for w in weights],
-        out_specs=(
-            pl.BlockSpec((count, length, width), lambda i: (i, 0, 0)),
-            pl.BlockSpec((2, 8, width), lambda i: (0, 0, 0)),
-        ),
-        compiler_params=pltpu.CompilerParams(vmem_limit_bytes=60 * 2**20),
-        name="layer%d" % level,
-    )(x, pos, *weights)
-
-
-def global_norm(rows, stats, gain, bias, shards):
-    cells = float(rows.size * shards)
-    sums = lax.psum(jnp.sum(stats, axis=(1, 2)), "span")
-    center = sums[0] / cells
-    spread = sums[1] / cells - center * center
-    return gain * (rows.astype(F32) - center) * lax.rsqrt(spread + norm_eps) + bias
-
-
-def body(mixture, wq, wk, wv, wo, wu, wd, ln, gln_gain, gln_bias):
-    shards = lax.axis_size("span")
-    weights = (wq, wk, wv, wo, wu, wd, ln)
-    intra, stats = run_layer(mixture, 0, weights)
-    intra_out = (
-        global_norm(intra, stats, gln_gain[0], gln_bias[0], shards) + mixture.astype(F32)
-    ).astype(BF16)
-    moved = lax.all_to_all(intra_out, "span", split_axis=1, concat_axis=0, tiled=True)
-    inter, stats = run_layer(jnp.swapaxes(moved, 0, 1), 1, weights)
-    back = lax.all_to_all(inter, "span", split_axis=1, concat_axis=0, tiled=True)
-    final = global_norm(back, stats, gln_gain[1], gln_bias[1], shards)
-    return (jnp.swapaxes(final, 0, 1) + intra_out.astype(F32)).astype(BF16)
+        name="dual_path",
+    )(mix, *weights, ln, gln_gain, gln_bias, pos0, pos1)
+    return result.reshape(mixture.shape)
 
 
 def solution(mesh):

time: 176 us -> 98.2 us (0.56)
  blocking collectives: 77 us -> 0 us
  Pallas kernels: 71.3 us -> 95 us
  other arithmetic: 8.71 us -> 0 us
  local copies, waits for them, and re-layouts: 9.21 us -> 3.1 us
  between operations: 4.92 us -> 0.01 us
  starting transfers between devices: 4.34 us -> 0 us
    psum x2 -> x0, blocking collectives: 48 us -> none  [global_norm(): sums = lax.psum(jnp.sum(stats, axis=(1, 2)), 'span')]
    all_to_all x1 -> x0, blocking collectives: 29 us -> none  [body(): lax.all_to_all(intra_out, 'span', split_axis=1, concat_axis=0, tiled=True)]
    pallas_call x2 -> x1, Pallas kernels: 71.3 us -> 95 us  [body(): pl.pallas_call(lambda *r: block_kernel(n, halves, *r), out_shape=jax.Shap...]
    convert_element_type x2 -> x0, other arithmetic: 5.6 us -> none  [the longest x1 3.24 us: body(): intra_out = (global_norm(intra, stats, gln_gain[0], gln_bias[0], shards)...]
    all_to_all x1 -> x0, starting transfers between devices: 4.34 us -> none  [body(): lax.all_to_all(inter, 'span', split_axis=1, concat_axis=0, tiled=True)]
    pallas_call x1 -> x0, local copies, waits for them, and re-layouts: 4.1 us -> none  [run_layer(): pl.pallas_call(lambda *r: layer_kernel(level, *r), grid=(total // count,)...]
    unnamed x4 -> x1, local copies, waits for them, and re-layouts: 0.01 us -> 3.1 us
    sub x1 -> x0, other arithmetic: 2.2 us -> none  [global_norm(): rows.astype(F32) - center]
  transfers between devices with their start and end apart: 1 -> 0, of which waited for: 0 -> 0; matrix products, arithmetic and copies ran while one was open for 0% -> 0% of each run, Pallas kernels for 0% -> 0%
where the time goes in v2:
time: 98.2 us; the launch traced here: 98.1 us
  Pallas kernels  95 us (97%)
  local copies, waits for them, and re-layouts  3.1 us (3%)
    pallas_call x1, Pallas kernels, body(): pl.pallas_call(lambda *r: block_kernel(n, halves, *r), out_shape=jax.Shap...  95 us
    unnamed x1, local copies, waits for them, and re-layouts  3.1 us

profile of v2, /device:TPU:0, one launch (start us, length us, event | category | flops | bytes accessed | tf_op | source)
XLA Modules:
  0.0 98.1 jit_solution(12020680525987953063)
XLA Ops:
  0.0 95.0 %dual_path.1 = bf16[16,16,16,256]{3,2,1,0:T(8,128)(2,1)} custom-call(bf16[16,16,16,256]{3,2,1,0:T(8,128)(2,1)} %bitcast.3, bf16[2,256,256]{2,1,0:T(8,128)(2,1)} %r_1_.1, bf16[2,256,256]{2,1,0:T(8,128)(2,1)} %r_2_.1, bf16[2,256,256]{2,1,0:T(8,128)(2,1)} %r_3_.1, bf16[2,256,256]{2,1,0:T(8,128)(2,1)} %r_4_.1, bf16[2,256,1024]{2,1,0:T(8,128)(2,1)} %r_5_.1, ...), custom_call_target="tpu_custom_call" | custom-call | tf_op jit(solution)/shard_map/dual_path/pallas_call | solution.py:363
  95.0 3.1 %copy.14 = bf16[16,256,256]{2,1,0:T(8,128)(2,1)} copy(bf16[16,256,256]{2,1,0:T(8,128)(2,1)} %bitcast.2) | data formatting | bytes 4194304

commit v3 on v2

--- a/solution.py
+++ b/solution.py
@@ -37,43 +37,51 @@
     return lax.dot_general(a, b, (((1,), (1,)), ((), ())), preferred_element_type=F32)
 
 
-def softmax_rows(scores, factor):
+def powers_of(scores, factor):
     top = jnp.max(scores, axis=-1, keepdims=True)
-    powers = jnp.exp2((scores - top) * factor)
-    return (powers * (1.0 / jnp.sum(powers, axis=-1, keepdims=True))).astype(BF16)
+    return jnp.exp2((scores - top) * factor).astype(BF16)
 
 
 def attend(q, k, v):
     length, width = q.shape
     head_dim = width // HEADS
+    side = width // 2
     factor = math.log2(math.e) / math.sqrt(head_dim)
     lane_head = lax.broadcasted_iota(jnp.int32, (1, width), 1) // head_dim
+    side_head = lax.broadcasted_iota(jnp.int32, (1, side), 1) // head_dim
+    per_side = HEADS // 2
 
     def mask(test):
         return jnp.where(test, 1.0, 0.0).astype(BF16)
 
-    total = None
-    if length * 2 <= width and length % 128 == 0:
-        half = HEADS // 2
+    def values_of(h):
+        own = mask(side_head == h % per_side)
+        start = (h // per_side) * side
+        ones = jnp.broadcast_to(own, (length, side))
+        return jnp.concatenate([v[:, start : start + side] * own, ones], axis=1)
+
+    paired = length * 2 <= width and length % 128 == 0
+    if paired:
         k_two = jnp.concatenate(
-            [k * mask(lane_head < half), k * mask(lane_head >= half)], axis=0
-        )
-        for h in range(half):
-            low, high = mask(lane_head == h), mask(lane_head == h + half)
-            scores = dot_nt(q * (low + high), k_two)
-            weights = jnp.concatenate(
-                [softmax_rows(scores[:, :length], factor), softmax_rows(scores[:, length:], factor)],
-                axis=1,
-            )
-            part = dot(weights, jnp.concatenate([v * low, v * high], axis=0))
+            [k * mask(lane_head % 2 == 0), k * mask(lane_head % 2 == 1)], axis=0
+        )
+    contexts = []
+    for first in (0, per_side):
+        total = None
+        for h in range(first, first + per_side, 2 if paired else 1):
+            if paired:
+                scores = dot_nt(q * mask(lane_head // 2 == h // 2), k_two)
+                weights = jnp.concatenate(
+                    [powers_of(scores[:, :length], factor), powers_of(scores[:, length:], factor)],
+                    axis=1,
+                )
+                part = dot(weights, jnp.concatenate([values_of(h), values_of(h + 1)], axis=0))
+            else:
+                weights = powers_of(dot_nt(q * mask(lane_head == h), k), factor)
+                part = dot(weights, values_of(h))
             total = part if total is None else total + part
-    else:
-        for h in range(HEADS):
-            own = mask(lane_head == h)
-            weights = softmax_rows(dot_nt(q * own, k), factor)
-            part = dot(weights, v * own)
-            total = part if total is None else total + part
-    return total.astype(BF16)
+        contexts.append((total[:, :side] / total[:, side:]).astype(BF16))
+    return jnp.concatenate(contexts, axis=1)
 
 
 def layer_rows(x, count, level, refs):
@@ -234,10 +242,13 @@
     first.wait()
     for load in loads[0]:
         load.wait()
-    later.wait()
     refs = (wq, wk, wv, wo, wu, wd, ln)
 
     def intra_step(i, carry):
+        @pl.when(i == 1)
+        def _():
+            later.wait()
+
         @pl.when(i > 0)
         def _():
             for j in range(1, n):

time: 98.2 us -> 96.6 us (0.984)
  Pallas kernels: 95 us -> 93.3 us
    pallas_call x1, Pallas kernels: 95 us -> 93.3 us  [body(): pl.pallas_call(lambda *r: block_kernel(n, halves, *r), out_shape=jax.Shap...]
where the time goes in v3:
time: 96.6 us; the launch traced here: 96.4 us
  Pallas kernels  93.3 us (97%)
  local copies, waits for them, and re-layouts  3.1 us (3%)
    pallas_call x1, Pallas kernels, body(): pl.pallas_call(lambda *r: block_kernel(n, halves, *r), out_shape=jax.Shap...  93.3 us
    unnamed x1, local copies, waits for them, and re-layouts  3.1 us

profile of v3, /device:TPU:0, one launch (start us, length us, event | category | flops | bytes accessed | tf_op | source)
XLA Modules:
  0.0 96.4 jit_solution(11150171152690424921)
XLA Ops:
  0.0 93.3 %dual_path.1 = bf16[16,16,16,256]{3,2,1,0:T(8,128)(2,1)} custom-call(bf16[16,16,16,256]{3,2,1,0:T(8,128)(2,1)} %bitcast.3, bf16[2,256,256]{2,1,0:T(8,128)(2,1)} %r_1_.1, bf16[2,256,256]{2,1,0:T(8,128)(2,1)} %r_2_.1, bf16[2,256,256]{2,1,0:T(8,128)(2,1)} %r_3_.1, bf16[2,256,256]{2,1,0:T(8,128)(2,1)} %r_4_.1, bf16[2,256,1024]{2,1,0:T(8,128)(2,1)} %r_5_.1, ...), custom_call_target="tpu_custom_call" | custom-call | tf_op jit(solution)/shard_map/dual_path/pallas_call | solution.py:374
  93.3 3.1 %copy.14 = bf16[16,256,256]{2,1,0:T(8,128)(2,1)} copy(bf16[16,256,256]{2,1,0:T(8,128)(2,1)} %bitcast.2) | data formatting | bytes 4194304
